TPU v7x, 32 devices: a whole 2x2x4 slice. The times are simulated.
32 devices in a mesh: hist: 16 (over z, x, core), orb: 2 (over y).
Axes of the slice: x: 2, y: 2, z: 4, core: 2. Of those that a mesh axis runs over, the one named last changes fastest.
Arguments:
- g_hist: bfloat16 [32, 64, 2048], P('hist', 'orb'), may hold values from -6 to 6
- sigma_hist: bfloat16 [2, 64, 2048], P(None, None, 'hist'), may hold values from -0.125 to 0.125
- diag_inv: float32 [32, 64, 64], P('hist'), may hold values from -0.75 to 0.75
- previous: float32 [2, 32, 64, 64], P(None, 'hist', 'orb'), may hold values from -6 to 6
- block_of_slot: int32 [16], replicated, may hold values from 0 to 15, each once
- front_pos: int32 [2], replicated, may hold values from 16 to 31
Outputs:
- g_row: float32 [2, 32, 64, 64], P(None, 'hist', 'orb')
- sigma_row: float32 [2, 32, 64, 64], P(None, 'hist', 'orb')
Inputs may be any that keep to these rules, and one draw needn't show every extreme that they name: `block_of_slot`: every block index appears once.
All inputs are finite; a program needn't handle non-finite values.
Results may differ from a plain program's by a relative error of at most 0.0003.
Values may be sent and summed in bfloat16 or wider, within the bound.
A program may use at most 64 MiB of HBM per device.

v0:
```python
import jax
import jax.numpy as jnp
from jax import lax
from jax.sharding import PartitionSpec as P

COUPLING = 0.5


def broadcast(value, axis, root):
    mine = lax.axis_index(axis) == root
    return lax.psum(jnp.where(mine, value, jnp.zeros_like(value)), axis)


def contract(g_piece, s_piece, times, col_time, front_pos):
    g_kept = jnp.where(
        (times[None, :] >= col_time[:, None])[:, None, :], g_piece, jnp.zeros_like(g_piece)
    )
    s_kept = jnp.where(
        (times[None, :] <= front_pos[:, None])[:, None, :], s_piece, jnp.zeros_like(s_piece)
    )
    return jnp.einsum("tcx,fax->ftca", g_kept, s_kept, preferred_element_type=jnp.float32)


def inverse_row(diag_inv, when, col_count):
    local = lax.dynamic_index_in_dim(diag_inv, when % col_count, 0, keepdims=False)
    return broadcast(local, "hist", when // col_count)


def body(g_hist, sigma_hist, diag_inv, previous, block_of_slot, front_pos):
    col_count = g_hist.shape[0]
    half_cols = g_hist.shape[1]
    orb_width = sigma_hist.shape[1]
    orb_id = lax.axis_index("orb")
    slot_id = lax.axis_index("hist")
    my_block = lax.dynamic_index_in_dim(block_of_slot, slot_id, 0, keepdims=False)
    col_time = my_block * col_count + jnp.arange(col_count, dtype=jnp.int32)
    piece = lax.all_gather(sigma_hist, "hist", axis=2, tiled=True)
    count = piece.shape[2]
    times = jnp.arange(count, dtype=jnp.int32) // orb_width
    integral = contract(g_hist, piece, times, col_time, front_pos)
    combined = previous + integral
    rows = jnp.stack([inverse_row(diag_inv, front_pos[front], col_count) for front in range(2)])
    g_row = jnp.einsum("ftcb,fab->ftca", combined, rows, precision=lax.Precision.HIGHEST)
    whole = lax.all_gather(g_row, "orb", axis=2, tiled=True)
    mirror = jnp.swapaxes(lax.dynamic_slice_in_dim(whole, orb_id * half_cols, half_cols, 3), 2, 3)
    sigma_row = COUPLING * g_row * g_row * mirror
    return (g_row, sigma_row)


def solution(mesh):
    in_specs = (
        P("hist", "orb", None),
        P(None, None, "hist"),
        P("hist", None, None),
        P(None, "hist", "orb", None),
        P(),
        P(),
    )
    out_specs = (P(None, "hist", "orb", None), P(None, "hist", "orb", None))
    return jax.shard_map(body, mesh=mesh, in_specs=in_specs, out_specs=out_specs, check_vma=False)
```

profile of v0, /device:TPU:0, one launch (start us, length us, event | category | flops | bytes accessed | tf_op | source)
XLA Modules:
  0.0 99.1 jit_solution(8734970899965628988)
XLA Ops:
  0.6 0.0 copy-start.4
  0.6 0.0 copy-start.3
  0.6 25.0 %all_gather.6 = bf16[2,64,2048]{2,1,0:T(8,128)(2,1)S(1)} all-gather(bf16[2,64,128]{2,1,0:T(8,128)(2,1)} %param.7), channel_id=1, replica_groups=mesh['hist'=16,'orb'=2] {'hist'}, dimensions={2}, use_global_device_ids=true | all-gather | bytes 557056 | tf_op jit(solution)/shard_map/all_gather | solution.py:37
  25.6 0.0 copy-start.5
  25.6 0.7 copy-done.5
  26.3 0.6 dynamic_slice.14
  27.5 0.0 copy-start.2
  27.5 0.6 copy-done.2
  28.2 0.1 broadcast_compare_fusion
  28.3 0.0 copy-done.4
  28.3 0.0 copy-done.3
  28.3 0.4 fusion
  28.7 0.0 copy-start.1
  28.7 0.6 fusion.18
  34.5 0.0 copy-done.1
  34.5 57.9 %all-reduce = (f32[1,64,64]{2,1,0:T(8,128)S(1)}, f32[1,64,64]{2,1,0:T(8,128)S(1)}) all-reduce(f32[1,64,64]{2,1,0:T(8,128)S(1)} %get-tuple-element.7, f32[1,64,64]{2,1,0:T(8,128)S(1)} %get-tuple-element.6), channel_id=1, replica_groups=mesh['hist'=16,'orb'=2] {'hist'}, use_global_device_ids=true, to_apply=%region_1.2 | all-reduce | flops 8192 | bytes 65536 | tf_op jit(solution)/shard_map/psum | solution.py:11
  92.4 0.2 fusion.10
  92.7 0.0 copy-start
  92.7 0.1 copy.8
  92.8 0.5 copy-done
  93.3 4.9 %all_gather.7 = f32[2,2,64,64]{3,2,1,0:T(8,128)S(1)} all-gather(f32[2,2,32,64]{3,2,1,0:T(8,128)S(1)} %fusion.10), channel_id=1, replica_groups=mesh['hist'=16,'orb'=2] {'orb'}, dimensions={2}, use_global_device_ids=true | all-gather | bytes 98304 | tf_op jit(solution)/shard_map/all_gather | solution.py:44
  98.2 0.1 fusion.8
  98.3 0.7 copy.10
  (3 shorter events, 0.0 us)
Async XLA Ops:
  0.6 27.6 %copy-start.4 = (f32[2,2,32,64]{3,2,1,0:T(8,128)S(1)}, f32[2,2,32,64]{3,2,1,0:T(8,128)}, u32[]{:S(2)}) copy-start(f32[2,2,32,64]{3,2,1,0:T(8,128)} %param.9) | copy-start | bytes 98308
  0.6 27.6 %copy-start.3 = (bf16[2,32,2048]{2,1,0:T(8,128)(2,1)S(1)}, bf16[2,32,2048]{2,1,0:T(8,128)(2,1)}, u32[]{:S(2)}) copy-start(bf16[2,32,2048]{2,1,0:T(8,128)(2,1)} %param.6) | copy-start | bytes 786436
  25.6 0.7 copy-start.5
  27.5 0.7 copy-start.2
  28.7 5.8 %copy-start.1 = (f32[2,64,64]{2,1,0:T(8,128)S(1)}, f32[2,64,64]{2,1,0:T(8,128)}, u32[]{:S(2)}) copy-start(f32[2,64,64]{2,1,0:T(8,128)} %param.8) | copy-start | bytes 98308
  92.7 0.6 copy-start
where the time goes:
time: 99.3 us; the launch traced here: 99.1 us
  blocking collectives  87.8 us (88%)
  between operations  6.62 us (7%)
  local copies, waits for them, and re-layouts  3.81 us (4%)
    psum x1, blocking collectives, broadcast(): return lax.psum(jnp.where(mine, value, jnp.zeros_like(value)), axis)  57.9 us
    all_gather x1, blocking collectives, body(): piece = lax.all_gather(sigma_hist, 'hist', axis=2, tiled=True)  25 us
    all_gather x1, blocking collectives, body(): whole = lax.all_gather(g_row, 'orb', axis=2, tiled=True)  4.92 us
    unnamed x13, local copies, waits for them, and re-layouts  2.55 us

commit v1 on v0

--- a/solution.py
+++ b/solution.py
@@ -34,7 +34,12 @@
     slot_id = lax.axis_index("hist")
     my_block = lax.dynamic_index_in_dim(block_of_slot, slot_id, 0, keepdims=False)
     col_time = my_block * col_count + jnp.arange(col_count, dtype=jnp.int32)
-    piece = lax.all_gather(sigma_hist, "hist", axis=2, tiled=True)
+    ring = [sigma_hist]
+    for hop in range(15):
+        ring.append(lax.ppermute(ring[-1], "hist", [(dev, (dev + 1) % 16) for dev in range(16)]))
+    piece = jnp.roll(
+        jnp.concatenate(ring[::-1], axis=2), (lax.axis_index("hist") + 1) * ring[0].shape[2], axis=2
+    )
     count = piece.shape[2]
     times = jnp.arange(count, dtype=jnp.int32) // orb_width
     integral = contract(g_hist, piece, times, col_time, front_pos)

time: 99.3 us -> 158 us (1.59)
  waiting for transfers between devices: 0 us -> 77.4 us
  blocking collectives: 87.8 us -> 67 us
    ppermute x0 -> x15, waiting for transfers between devices: none -> 77.4 us  [body(): lax.ppermute(ring[-1], 'hist', [(dev, (dev + 1) % 16) for dev in range(16)])]
    all_gather x1 -> x0, blocking collectives: 25 us -> none  [body(): piece = lax.all_gather(sigma_hist, 'hist', axis=2, tiled=True)]
    psum x1, blocking collectives: 57.9 us -> 62 us  [broadcast(): return lax.psum(jnp.where(mine, value, jnp.zeros_like(value)), axis)]
    unnamed x13 -> x46, local copies, waits for them, and re-layouts: 2.55 us -> 3.36 us
  transfers between devices with their start and end apart: 0 -> 15, of which waited for: 0 -> 14; matrix products, arithmetic and copies ran while one was open for 0% -> 1% of each run, Pallas kernels for 0% -> 0%
where the time goes in v1:
time: 158 us; the launch traced here: 157 us
  waiting for transfers between devices  77.4 us (49%)
  blocking collectives  67 us (42%)
  between operations  6.8 us (4%)
  local copies, waits for them, and re-layouts  4.63 us (3%)
    ppermute x15, waiting for transfers between devices, body(): lax.ppermute(ring[-1], 'hist', [(dev, (dev + 1) % 16) for dev in range(16)])  77.4 us
    psum x1, blocking collectives, broadcast(): return lax.psum(jnp.where(mine, value, jnp.zeros_like(value)), axis)  62 us
    all_gather x1, blocking collectives, body(): whole = lax.all_gather(g_row, 'orb', axis=2, tiled=True)  4.93 us
    unnamed x46, local copies, waits for them, and re-layouts  3.36 us
  transfers between devices with their start and end apart: 15, of which 14 were waited for; matrix products, arithmetic and copies ran while one was open for 1% of the time, Pallas kernels for 0%

profile of v1, /device:TPU:0, one launch (start us, length us, event | category | flops | bytes accessed | tf_op | source)
XLA Modules:
  0.0 157.2 jit_solution(4675046525050747533)
XLA Ops:
  0.6 0.5 collective-permute-start
  1.2 6.8 %collective-permute-done = bf16[2,64,128]{2,1,0:T(8,128)(2,1)S(1)} collective-permute-done((bf16[2,64,128]{2,1,0:T(8,128)(2,1)}, bf16[2,64,128]{2,1,0:T(8,128)(2,1)S(1)}, u32[]{:S(2)}, u32[]{:S(2)}) %collective-permute-start) | collective-permute-done | bytes 32800 | tf_op jit(solution)/shard_map/ppermute | solution.py:39
  7.9 6.0 %collective-permute-done.1 = bf16[2,64,128]{2,1,0:T(8,128)(2,1)S(1)} collective-permute-done((bf16[2,64,128]{2,1,0:T(8,128)(2,1)S(1)}, bf16[2,64,128]{2,1,0:T(8,128)(2,1)S(1)}, u32[]{:S(2)}, u32[]{:S(2)}) %collective-permute-start.1) | collective-permute-done | bytes 32800 | tf_op jit(solution)/shard_map/ppermute | solution.py:39
  14.0 6.0 %collective-permute-done.2 = bf16[2,64,128]{2,1,0:T(8,128)(2,1)S(1)} collective-permute-done((bf16[2,64,128]{2,1,0:T(8,128)(2,1)S(1)}, bf16[2,64,128]{2,1,0:T(8,128)(2,1)S(1)}, u32[]{:S(2)}, u32[]{:S(2)}) %collective-permute-start.2) | collective-permute-done | bytes 32800 | tf_op jit(solution)/shard_map/ppermute | solution.py:39
  20.0 6.0 %collective-permute-done.3 = bf16[2,64,128]{2,1,0:T(8,128)(2,1)S(1)} collective-permute-done((bf16[2,64,128]{2,1,0:T(8,128)(2,1)S(1)}, bf16[2,64,128]{2,1,0:T(8,128)(2,1)S(1)}, u32[]{:S(2)}, u32[]{:S(2)}) %collective-permute-start.3) | collective-permute-done | bytes 32800 | tf_op jit(solution)/shard_map/ppermute | solution.py:39
  26.1 6.0 %collective-permute-done.4 = bf16[2,64,128]{2,1,0:T(8,128)(2,1)S(1)} collective-permute-done((bf16[2,64,128]{2,1,0:T(8,128)(2,1)S(1)}, bf16[2,64,128]{2,1,0:T(8,128)(2,1)S(1)}, u32[]{:S(2)}, u32[]{:S(2)}) %collective-permute-start.4) | collective-permute-done | bytes 32800 | tf_op jit(solution)/shard_map/ppermute | solution.py:39
  32.1 6.0 %collective-permute-done.5 = bf16[2,64,128]{2,1,0:T(8,128)(2,1)S(1)} collective-permute-done((bf16[2,64,128]{2,1,0:T(8,128)(2,1)S(1)}, bf16[2,64,128]{2,1,0:T(8,128)(2,1)S(1)}, u32[]{:S(2)}, u32[]{:S(2)}) %collective-permute-start.5) | collective-permute-done | bytes 32800 | tf_op jit(solution)/shard_map/ppermute | solution.py:39
  38.1 6.0 %collective-permute-done.6 = bf16[2,64,128]{2,1,0:T(8,128)(2,1)S(1)} collective-permute-done((bf16[2,64,128]{2,1,0:T(8,128)(2,1)S(1)}, bf16[2,64,128]{2,1,0:T(8,128)(2,1)S(1)}, u32[]{:S(2)}, u32[]{:S(2)}) %collective-permute-start.6) | collective-permute-done | bytes 32800 | tf_op jit(solution)/shard_map/ppermute | solution.py:39
  44.2 6.0 %collective-permute-done.7 = bf16[2,64,128]{2,1,0:T(8,128)(2,1)S(1)} collective-permute-done((bf16[2,64,128]{2,1,0:T(8,128)(2,1)S(1)}, bf16[2,64,128]{2,1,0:T(8,128)(2,1)S(1)}, u32[]{:S(2)}, u32[]{:S(2)}) %collective-permute-start.7) | collective-permute-done | bytes 32800 | tf_op jit(solution)/shard_map/ppermute | solution.py:39
  50.2 6.0 %collective-permute-done.8 = bf16[2,64,128]{2,1,0:T(8,128)(2,1)S(1)} collective-permute-done((bf16[2,64,128]{2,1,0:T(8,128)(2,1)S(1)}, bf16[2,64,128]{2,1,0:T(8,128)(2,1)S(1)}, u32[]{:S(2)}, u32[]{:S(2)}) %collective-permute-start.8) | collective-permute-done | bytes 32800 | tf_op jit(solution)/shard_map/ppermute | solution.py:39
  56.2 6.0 %collective-permute-done.9 = bf16[2,64,128]{2,1,0:T(8,128)(2,1)S(1)} collective-permute-done((bf16[2,64,128]{2,1,0:T(8,128)(2,1)S(1)}, bf16[2,64,128]{2,1,0:T(8,128)(2,1)S(1)}, u32[]{:S(2)}, u32[]{:S(2)}) %collective-permute-start.9) | collective-permute-done | bytes 32800 | tf_op jit(solution)/shard_map/ppermute | solution.py:39
  62.3 0.7 copy-done.6
  62.9 0.6 dynamic_slice.19
  64.2 4.1 %collective-permute-done.10 = bf16[2,64,128]{2,1,0:T(8,128)(2,1)S(1)} collective-permute-done((bf16[2,64,128]{2,1,0:T(8,128)(2,1)S(1)}, bf16[2,64,128]{2,1,0:T(8,128)(2,1)S(1)}, u32[]{:S(2)}, u32[]{:S(2)}) %collective-permute-start.10) | collective-permute-done | bytes 32800 | tf_op jit(solution)/shard_map/ppermute | solution.py:39
  68.3 6.0 %collective-permute-done.11 = bf16[2,64,128]{2,1,0:T(8,128)(2,1)S(1)} collective-permute-done((bf16[2,64,128]{2,1,0:T(8,128)(2,1)S(1)}, bf16[2,64,128]{2,1,0:T(8,128)(2,1)S(1)}, u32[]{:S(2)}, u32[]{:S(2)}) %collective-permute-start.11) | collective-permute-done | bytes 32800 | tf_op jit(solution)/shard_map/ppermute | solution.py:39
  74.4 5.9 %collective-permute-done.12 = bf16[2,64,128]{2,1,0:T(8,128)(2,1)S(1)} collective-permute-done((bf16[2,64,128]{2,1,0:T(8,128)(2,1)S(1)}, bf16[2,64,128]{2,1,0:T(8,128)(2,1)S(1)}, u32[]{:S(2)}, u32[]{:S(2)}) %collective-permute-start.12) | collective-permute-done | bytes 32800 | tf_op jit(solution)/shard_map/ppermute | solution.py:39
  80.4 0.6 fusion.20
  86.2 0.2 collective-permute-done.13
  86.5 62.0 %all-reduce = (f32[1,64,64]{2,1,0:T(8,128)S(1)}, f32[1,64,64]{2,1,0:T(8,128)S(1)}) all-reduce(f32[1,64,64]{2,1,0:T(8,128)S(1)} %get-tuple-element.7, f32[1,64,64]{2,1,0:T(8,128)S(1)} %get-tuple-element.6), channel_id=1, replica_groups=mesh['hist'=16,'orb'=2] {'hist'}, use_global_device_ids=true, to_apply=%region_1.2 | all-reduce | flops 8192 | bytes 65536 | tf_op jit(solution)/shard_map/psum | solution.py:11
  148.8 0.7 copy-done.1
  149.9 0.8 copy-done.4
  150.7 0.4 fusion
  151.3 4.9 %all_gather.3 = f32[2,2,64,64]{3,2,1,0:T(8,128)S(1)} all-gather(f32[2,2,32,64]{3,2,1,0:T(8,128)S(1)} %fusion.11), channel_id=1, replica_groups=mesh['hist'=16,'orb'=2] {'orb'}, dimensions={2}, use_global_device_ids=true | all-gather | bytes 98304 | tf_op jit(solution)/shard_map/all_gather | solution.py:49
  156.5 0.7 copy.10
  (65 shorter events, 1.1 us)
Async XLA Ops:
  0.6 7.3 %collective-permute-start = (bf16[2,64,128]{2,1,0:T(8,128)(2,1)}, bf16[2,64,128]{2,1,0:T(8,128)(2,1)S(1)}, u32[]{:S(2)}, u32[]{:S(2)}) collective-permute-start(bf16[2,64,128]{2,1,0:T(8,128)(2,1)} %param.7), channel_id=1, source_target_pairs={{0,2},{2,4},{4,6},{6,8},{8,10},{10,12},{12,14},{14,16},{16,18},{18... | collective-permute-start | bytes 98312 | tf_op jit(solution)/shard_map/ppermute | solution.py:39
  7.9 6.0 %collective-permute-start.1 = (bf16[2,64,128]{2,1,0:T(8,128)(2,1)S(1)}, bf16[2,64,128]{2,1,0:T(8,128)(2,1)S(1)}, u32[]{:S(2)}, u32[]{:S(2)}) collective-permute-start(bf16[2,64,128]{2,1,0:T(8,128)(2,1)S(1)} %collective-permute-done), channel_id=1, source_target_pairs={{0,2},{2,4},{4,6},{6,8},{8,10},{10,12},{12,14},{14,16},{16,18},{18... | collective-permute-start | bytes 98312 | tf_op jit(solution)/shard_map/ppermute | solution.py:39
  14.0 6.0 %collective-permute-start.2 = (bf16[2,64,128]{2,1,0:T(8,128)(2,1)S(1)}, bf16[2,64,128]{2,1,0:T(8,128)(2,1)S(1)}, u32[]{:S(2)}, u32[]{:S(2)}) collective-permute-start(bf16[2,64,128]{2,1,0:T(8,128)(2,1)S(1)} %collective-permute-done.1), channel_id=1, source_target_pairs={{0,2},{2,4},{4,6},{6,8},{8,10},{10,12},{12,14},{14,16},{16,18},{18... | collective-permute-start | bytes 98312 | tf_op jit(solution)/shard_map/ppermute | solution.py:39
  20.0 6.0 %collective-permute-start.3 = (bf16[2,64,128]{2,1,0:T(8,128)(2,1)S(1)}, bf16[2,64,128]{2,1,0:T(8,128)(2,1)S(1)}, u32[]{:S(2)}, u32[]{:S(2)}) collective-permute-start(bf16[2,64,128]{2,1,0:T(8,128)(2,1)S(1)} %collective-permute-done.2), channel_id=1, source_target_pairs={{0,2},{2,4},{4,6},{6,8},{8,10},{10,12},{12,14},{14,16},{16,18},{18... | collective-permute-start | bytes 98312 | tf_op jit(solution)/shard_map/ppermute | solution.py:39
  26.1 6.0 %collective-permute-start.4 = (bf16[2,64,128]{2,1,0:T(8,128)(2,1)S(1)}, bf16[2,64,128]{2,1,0:T(8,128)(2,1)S(1)}, u32[]{:S(2)}, u32[]{:S(2)}) collective-permute-start(bf16[2,64,128]{2,1,0:T(8,128)(2,1)S(1)} %collective-permute-done.3), channel_id=1, source_target_pairs={{0,2},{2,4},{4,6},{6,8},{8,10},{10,12},{12,14},{14,16},{16,18},{18... | collective-permute-start | bytes 98312 | tf_op jit(solution)/shard_map/ppermute | solution.py:39
  32.1 6.0 %collective-permute-start.5 = (bf16[2,64,128]{2,1,0:T(8,128)(2,1)S(1)}, bf16[2,64,128]{2,1,0:T(8,128)(2,1)S(1)}, u32[]{:S(2)}, u32[]{:S(2)}) collective-permute-start(bf16[2,64,128]{2,1,0:T(8,128)(2,1)S(1)} %collective-permute-done.4), channel_id=1, source_target_pairs={{0,2},{2,4},{4,6},{6,8},{8,10},{10,12},{12,14},{14,16},{16,18},{18... | collective-permute-start | bytes 98312 | tf_op jit(solution)/shard_map/ppermute | solution.py:39
  38.1 6.0 %collective-permute-start.6 = (bf16[2,64,128]{2,1,0:T(8,128)(2,1)S(1)}, bf16[2,64,128]{2,1,0:T(8,128)(2,1)S(1)}, u32[]{:S(2)}, u32[]{:S(2)}) collective-permute-start(bf16[2,64,128]{2,1,0:T(8,128)(2,1)S(1)} %collective-permute-done.5), channel_id=1, source_target_pairs={{0,2},{2,4},{4,6},{6,8},{8,10},{10,12},{12,14},{14,16},{16,18},{18... | collective-permute-start | bytes 98312 | tf_op jit(solution)/shard_map/ppermute | solution.py:39
  44.2 6.0 %collective-permute-start.7 = (bf16[2,64,128]{2,1,0:T(8,128)(2,1)S(1)}, bf16[2,64,128]{2,1,0:T(8,128)(2,1)S(1)}, u32[]{:S(2)}, u32[]{:S(2)}) collective-permute-start(bf16[2,64,128]{2,1,0:T(8,128)(2,1)S(1)} %collective-permute-done.6), channel_id=1, source_target_pairs={{0,2},{2,4},{4,6},{6,8},{8,10},{10,12},{12,14},{14,16},{16,18},{18... | collective-permute-start | bytes 98312 | tf_op jit(solution)/shard_map/ppermute | solution.py:39
  50.2 6.0 %collective-permute-start.8 = (bf16[2,64,128]{2,1,0:T(8,128)(2,1)S(1)}, bf16[2,64,128]{2,1,0:T(8,128)(2,1)S(1)}, u32[]{:S(2)}, u32[]{:S(2)}) collective-permute-start(bf16[2,64,128]{2,1,0:T(8,128)(2,1)S(1)} %collective-permute-done.7), channel_id=1, source_target_pairs={{0,2},{2,4},{4,6},{6,8},{8,10},{10,12},{12,14},{14,16},{16,18},{18... | collective-permute-start | bytes 98312 | tf_op jit(solution)/shard_map/ppermute | solution.py:39
  56.2 6.0 %collective-permute-start.9 = (bf16[2,64,128]{2,1,0:T(8,128)(2,1)S(1)}, bf16[2,64,128]{2,1,0:T(8,128)(2,1)S(1)}, u32[]{:S(2)}, u32[]{:S(2)}) collective-permute-start(bf16[2,64,128]{2,1,0:T(8,128)(2,1)S(1)} %collective-permute-done.8), channel_id=1, source_target_pairs={{0,2},{2,4},{4,6},{6,8},{8,10},{10,12},{12,14},{14,16},{16,18},{18... | collective-permute-start | bytes 98312 | tf_op jit(solution)/shard_map/ppermute | solution.py:39
  62.3 6.0 %collective-permute-start.10 = (bf16[2,64,128]{2,1,0:T(8,128)(2,1)S(1)}, bf16[2,64,128]{2,1,0:T(8,128)(2,1)S(1)}, u32[]{:S(2)}, u32[]{:S(2)}) collective-permute-start(bf16[2,64,128]{2,1,0:T(8,128)(2,1)S(1)} %collective-permute-done.9), channel_id=1, source_target_pairs={{0,2},{2,4},{4,6},{6,8},{8,10},{10,12},{12,14},{14,16},{16,18},{18... | collective-permute-start | bytes 98312 | tf_op jit(solution)/shard_map/ppermute | solution.py:39
  62.3 0.7 copy-start.6
  62.9 11.4 %copy-start.3 = (s32[2]{0:T(128)S(1)}, s32[2]{0:T(128)}, u32[]{:S(2)}) copy-start(s32[2]{0:T(128)} %param.11) | copy-start | bytes 28
  63.5 22.9 %copy-start.2 = (f32[2,64,64]{2,1,0:T(8,128)S(1)}, f32[2,64,64]{2,1,0:T(8,128)}, u32[]{:S(2)}) copy-start(f32[2,64,64]{2,1,0:T(8,128)} %param.8) | copy-start | bytes 98308
  68.3 6.0 %collective-permute-start.11 = (bf16[2,64,128]{2,1,0:T(8,128)(2,1)S(1)}, bf16[2,64,128]{2,1,0:T(8,128)(2,1)S(1)}, u32[]{:S(2)}, u32[]{:S(2)}) collective-permute-start(bf16[2,64,128]{2,1,0:T(8,128)(2,1)S(1)} %collective-permute-done.10), channel_id=1, source_target_pairs={{0,2},{2,4},{4,6},{6,8},{8,10},{10,12},{12,14},{14,16},{16,18},{18... | collective-permute-start | bytes 98312 | tf_op jit(solution)/shard_map/ppermute | solution.py:39
  74.3 6.0 %collective-permute-start.12 = (bf16[2,64,128]{2,1,0:T(8,128)(2,1)S(1)}, bf16[2,64,128]{2,1,0:T(8,128)(2,1)S(1)}, u32[]{:S(2)}, u32[]{:S(2)}) collective-permute-start(bf16[2,64,128]{2,1,0:T(8,128)(2,1)S(1)} %collective-permute-done.11), channel_id=1, source_target_pairs={{0,2},{2,4},{4,6},{6,8},{8,10},{10,12},{12,14},{14,16},{16,18},{18... | collective-permute-start | bytes 98312 | tf_op jit(solution)/shard_map/ppermute | solution.py:39
  80.4 6.1 %collective-permute-start.13 = (bf16[2,64,128]{2,1,0:T(8,128)(2,1)S(1)}, bf16[2,64,128]{2,1,0:T(8,128)(2,1)S(1)}, u32[]{:S(2)}, u32[]{:S(2)}) collective-permute-start(bf16[2,64,128]{2,1,0:T(8,128)(2,1)S(1)} %collective-permute-done.12), channel_id=1, source_target_pairs={{0,2},{2,4},{4,6},{6,8},{8,10},{10,12},{12,14},{14,16},{16,18},{18... | collective-permute-start | bytes 98312 | tf_op jit(solution)/shard_map/ppermute | solution.py:39
  86.4 62.1 %collective-permute-start.14 = (bf16[2,64,128]{2,1,0:T(8,128)(2,1)S(1)}, bf16[2,64,128]{2,1,0:T(8,128)(2,1)S(1)}, u32[]{:S(2)}, u32[]{:S(2)}) collective-permute-start(bf16[2,64,128]{2,1,0:T(8,128)(2,1)S(1)} %collective-permute-done.13), channel_id=1, source_target_pairs={{0,2},{2,4},{4,6},{6,8},{8,10},{10,12},{12,14},{14,16},{16,18},{18... | collective-permute-start | bytes 98312 | tf_op jit(solution)/shard_map/ppermute | solution.py:39
  148.8 0.8 copy-start.1
  149.7 1.0 copy-start.4
  149.8 0.9 copy-start.5
  151.3 4.9 %copy-start = (f32[2,2,32,64]{3,2,1,0:T(8,128)}, f32[2,2,32,64]{3,2,1,0:T(8,128)S(1)}, u32[]{:S(2)}) copy-start(f32[2,2,32,64]{3,2,1,0:T(8,128)S(1)} %fusion.11) | copy-start | bytes 98308
